TPU v7x, 32 devices: a whole 2x2x4 slice. The times are simulated.
32 devices in a mesh: dp: 4 (over z), fsdp: 8 (over y, x, core).
Axes of the slice: x: 2, y: 2, z: 4, core: 2. Of those that a mesh axis runs over, the one named last changes fastest.
Arguments:
- replica_grads: bfloat16 [4, 8192, 4096], P('dp', 'fsdp'), may hold values from -4 to 4
- slot_table: int32 [32], replicated, may hold values from 0 to 39, as said below
- left_gram_state: float32 [40, 1, 4, 256, 1024], P('fsdp', None, 'dp')
- right_gram_state: float32 [40, 1, 4, 256, 1024], P('fsdp', None, 'dp')
- left_inverse_root: bfloat16 [40, 1, 4, 256, 1024], P('fsdp', None, 'dp')
- right_inverse_root: bfloat16 [40, 1, 4, 256, 1024], P('fsdp', None, 'dp')
Outputs:
- direction: bfloat16 [8, 4, 256, 4096], P('fsdp', 'dp')
- left_new: float32 [40, 1, 4, 256, 1024], P('fsdp', None, 'dp')
- right_new: float32 [40, 1, 4, 256, 1024], P('fsdp', None, 'dp')
Inputs may be any that keep to these rules, and one draw needn't show every extreme that they name: `slot_table`: the entries are distinct; slot v belongs to owner v // 5 of the flat shards' devices; some owner holds 5 blocks.
All inputs are finite; a program needn't handle non-finite values.
Results may differ from a plain program's by a relative error of at most 0.02.
Values may be sent and summed in bfloat16 or wider, within the bound.
A program may use at most 192 MiB of HBM per device.

v0:
```python
import jax
import jax.numpy as jnp
from jax import lax
from jax.sharding import PartitionSpec as P


def on_device(
    replica_grads,
    slot_table,
    left_gram_state,
    right_gram_state,
    left_inverse_root,
    right_inverse_root,
):
    slots_here = left_gram_state.shape[0]
    sub_blocks = left_gram_state.shape[1]
    strip_rows = left_gram_state.shape[3]
    block_size = left_gram_state.shape[4]
    band_rows = replica_grads.shape[1]
    model_width = replica_grads.shape[2]
    per_band = model_width // block_size
    shards = lax.axis_size("fsdp")
    groups = lax.axis_size("dp")
    total_slots = shards * slots_here
    block_count = slot_table.shape[0]
    band_index = lax.axis_index("fsdp")
    strip_index = lax.axis_index("dp")
    slot_indices = jnp.arange(total_slots, dtype=jnp.int32)
    summed = lax.psum_scatter(
        replica_grads[0].astype(jnp.float32).astype(jnp.bfloat16),
        "dp",
        scatter_dimension=0,
        tiled=True,
    )
    row_block = band_index * band_rows // block_size
    targets = lax.dynamic_slice_in_dim(slot_table, row_block * per_band, per_band, 0)
    chooser = (targets[:, None] == slot_indices[None, :]).astype(jnp.bfloat16)
    own_slots = band_index * slots_here + jnp.arange(slots_here, dtype=jnp.int32)
    holder = slot_table[None, :] == own_slots[:, None]
    occupied = jnp.any(holder, axis=1)
    block_of = jnp.sum(
        jnp.where(holder, jnp.arange(block_count, dtype=jnp.int32)[None, :], 0), axis=1
    )
    first_band = block_of // per_band * sub_blocks
    col_block = block_of % per_band
    all_bands = lax.all_gather(summed[None], "fsdp", axis=0, tiled=True)
    owned_rows = jax.vmap(
        lambda offset, column: lax.dynamic_slice(
            all_bands, (offset, 0, column * block_size), (sub_blocks, strip_rows, block_size)
        )
    )(first_band, col_block)
    owned_rows = owned_rows * occupied[:, None, None, None].astype(jnp.bfloat16)
    owned_rows = owned_rows.reshape(slots_here, sub_blocks, 1, strip_rows, block_size)
    entire = lax.all_gather(owned_rows, "dp", axis=2, tiled=True).reshape(
        slots_here, block_size, block_size
    )
    my_rows = owned_rows.reshape(slots_here, sub_blocks * strip_rows, block_size)
    left_gram = jnp.einsum("mrc,mnc->mrn", my_rows, entire, preferred_element_type=jnp.float32)
    left_new = left_gram_state + (left_gram / block_size).reshape(left_gram_state.shape)
    my_columns = lax.dynamic_index_in_dim(
        entire.reshape(slots_here, block_size, sub_blocks, groups, strip_rows),
        strip_index,
        3,
        keepdims=False,
    )
    my_columns = my_columns.reshape(slots_here, block_size, sub_blocks * strip_rows)
    right_gram = jnp.einsum("mnr,mnc->mrc", my_columns, entire, preferred_element_type=jnp.float32)
    right_new = right_gram_state + (right_gram / block_size).reshape(right_gram_state.shape)
    left_rows = left_inverse_root.reshape(slots_here, sub_blocks * strip_rows, block_size)
    mixed_rows = jnp.einsum(
        "mrn,mnc->mrc", left_rows, entire, preferred_element_type=jnp.float32
    ).astype(jnp.bfloat16)
    mixed_split = mixed_rows.reshape(
        slots_here, sub_blocks * strip_rows, sub_blocks, groups, strip_rows
    )
    result = jnp.einsum(
        "mrqjt,mqjtc->mrc",
        mixed_split,
        lax.all_gather(right_inverse_root, "dp", axis=2, tiled=True),
        preferred_element_type=jnp.float32,
    )
    outcome = result.astype(jnp.bfloat16).reshape(slots_here, sub_blocks, strip_rows, block_size)
    homeward = jax.vmap(
        lambda portion, offset: lax.dynamic_update_slice_in_dim(
            jnp.zeros((shards, strip_rows, block_size), jnp.bfloat16), portion, offset, 0
        ),
        out_axes=1,
    )(outcome, first_band)
    returned = lax.all_to_all(homeward, "fsdp", split_axis=0, concat_axis=0, tiled=True)
    picked = jnp.einsum(
        "cn,ntb->tcb",
        chooser,
        returned.reshape(total_slots, strip_rows, block_size),
        preferred_element_type=jnp.float32,
    ).astype(jnp.bfloat16)
    direction = picked.reshape(1, 1, strip_rows, model_width)
    return (direction, left_new, right_new)


def solution(mesh):
    placed = (
        P("dp", "fsdp", None),
        P(),
        P("fsdp", None, "dp", None, None),
        P("fsdp", None, "dp", None, None),
        P("fsdp", None, "dp", None, None),
        P("fsdp", None, "dp", None, None),
    )
    return jax.shard_map(
        on_device,
        mesh=mesh,
        in_specs=placed,
        out_specs=(
            P("fsdp", "dp", None, None),
            P("fsdp", None, "dp", None, None),
            P("fsdp", None, "dp", None, None),
        ),
        check_vma=False,
    )
```

profile of v0, /device:TPU:0, one launch (start us, length us, event | category | flops | bytes accessed | tf_op | source)
XLA Modules:
  0.0 976.8 jit_solution(10129963581104067872)
XLA Ops:
  7.2 0.7 reduce-scatter.2.cloned.1.call-update
  8.0 149.7 %reduce-scatter.2.cloned.1.call-done = bf16[256,4096]{1,0:T(8,128)(2,1)} async-done(((bf16[1024,4096]{1,0:T(8,128)(2,1)}), bf16[256,4096]{1,0:T(8,128)(2,1)}) %reduce-scatter.2.cloned.1.call-update) | async-done | bytes 2097168 | tf_op jit(solution)/shard_map/reduce_scatter | solution.py:29
  158.3 91.7 %all-gather.9.cloned.1.call-done = bf16[2048,4096]{1,0:T(8,128)(2,1)} async-done(((bf16[256,4096]{1,0:T(8,128)(2,1)}), bf16[2048,4096]{1,0:T(8,128)(2,1)}) %all-gather.9.cloned.1.call-update) | async-done | bytes 16777232 | tf_op jit(solution)/shard_map/all_gather | solution.py:46
  250.0 19.5 %while.2 = (s32[]{:T(128)}, bf16[8,256,4096]{2,1,0:T(8,128)(2,1)}, s32[5,3]{0,1:T(4,128)S(1)}, bf16[5,1,256,1024]{3,2,1,0:T(8,128)(2,1)}, s32[]{:T(128)}) while((s32[]{:T(128)}, bf16[8,256,4096]{2,1,0:T(8,128)(2,1)}, s32[5,3]{0,1:T(4,128)S(1)}, bf16[5,1,256,1024]{3,2,1,0:T(8,128)(2,1)}, s32[]{:T(128)}) %tuple.63), condition=%wide.while_cond, body=%wide.while_body.sunk | while | flops 2 | bytes 1049717 | solution.py:48
  250.6 3.3 bitcast_dynamic-update-slice_fusion.4
  254.5 3.3 bitcast_dynamic-update-slice_fusion.4
  258.4 3.3 bitcast_dynamic-update-slice_fusion.4
  262.2 3.3 bitcast_dynamic-update-slice_fusion.4
  266.1 3.3 bitcast_dynamic-update-slice_fusion.4
  269.4 3.5 bitcast_multiply_fusion.2
  273.5 183.4 %all-gather.5.cloned.1.call-done = bf16[5,1,4,256,1024]{4,3,1,0,2:T(8,128)(2,1)} async-done(((bf16[5,1,1,256,1024]{4,3,1,0,2:T(8,128)(2,1)}), bf16[5,1,4,256,1024]{4,3,1,0,2:T(8,128)(2,1)}) %all-gather.5.cloned.1.call-update) | async-done | bytes 10485776 | tf_op jit(solution)/shard_map/all_gather | solution.py:54
  457.0 17.4 %copy.48 = bf16[5,1,4,256,1024]{3,2,4,0,1:T(4,128)(2,1)} copy(bf16[5,1,4,256,1024]{4,3,1,0,2:T(8,128)(2,1)} %all-gather.5.cloned.1.call-done) | data formatting | bytes 20971520 | tf_op jit(solution)/shard_map/all_gather | solution.py:54
  474.3 17.6 %reshape.158 = bf16[5,1024,1024]{1,2,0:T(8,128)(2,1)} reshape(bf16[5,1,4,256,1024]{3,2,4,0,1:T(4,128)(2,1)} %copy.48) | data formatting | bytes 20971520 | tf_op jit(solution)/shard_map/reshape | solution.py:54
  491.9 8.5 fusion.16
  500.4 140.1 %all-gather.7.cloned.1.call-done = bf16[5,1,4,256,1024]{4,3,2,0,1:T(8,128)(2,1)} async-done(((bf16[5,1,1,256,1024]{4,3,2,0,1:T(8,128)(2,1)}), bf16[5,1,4,256,1024]{4,3,2,0,1:T(8,128)(2,1)}) %all-gather.7.cloned.1.call-update) | async-done | bytes 10485776 | tf_op jit(solution)/shard_map/all_gather | solution.py:79
  640.5 9.3 fusion.6
  649.8 7.4 broadcast_in_dim.18.clone
  657.1 52.1 %while.3 = (s32[]{:T(128)}, bf16[5,8,256,1024]{3,2,0,1:T(8,128)(2,1)}, s32[5,4]{0,1:T(4,128)S(1)}, bf16[5,1,256,1024]{3,2,1,0:T(8,128)(2,1)}, s32[]{:T(128)}, /*index=5*/s32[4]{0:T(128)S(1)}) while((s32[]{:T(128)}, bf16[5,8,256,1024]{3,2,0,1:T(8,128)(2,1)}, s32[5,4]{0,1:T(4,128)S(1)}, bf16[5,1,256,1024]{3,2,1,0:T(8,128)(2,1)}, s32[]{:T(128)}, ...), condition=%wide.while_cond.1, body=%wide.while_body.1.sunk | while | flops 262173 | bytes 2623166 | solution.py:84
  657.2 0.6 fusion.37
  657.8 3.3 and_reduce_fusion.2
  661.1 2.4 constant_dynamic-slice_fusion.9
  663.6 4.0 bitcast_dynamic-update-slice_fusion.5
  667.6 0.6 fusion.37
  668.2 3.3 and_reduce_fusion.2
  671.6 2.4 constant_dynamic-slice_fusion.9
  674.0 4.0 bitcast_dynamic-update-slice_fusion.5
  678.0 0.6 fusion.37
  678.7 3.3 and_reduce_fusion.2
  682.0 2.4 constant_dynamic-slice_fusion.9
  684.4 4.0 bitcast_dynamic-update-slice_fusion.5
  688.5 0.6 fusion.37
  689.1 3.3 and_reduce_fusion.2
  692.4 2.4 constant_dynamic-slice_fusion.9
  694.8 4.0 bitcast_dynamic-update-slice_fusion.5
  698.9 0.6 fusion.37
  699.5 3.3 and_reduce_fusion.2
  702.8 2.4 constant_dynamic-slice_fusion.9
  705.3 4.0 bitcast_dynamic-update-slice_fusion.5
  709.2 6.3 all-to-all-start
  715.6 9.7 copy.56
  725.3 17.9 %reshape_reshape.4 = bf16[5,1024,1,4,256]{4,3,1,0,2:T(4,128)(2,1)} reshape(bf16[5,1,4,256,1024]{4,3,2,0,1:T(8,128)(2,1)} %copy.56) | data formatting | bytes 20971520 | tf_op jit(solution)/shard_map/reshape;reshape | solution.py:61
  743.2 8.7 constant_dynamic-slice_fusion.3
  751.8 11.1 %copy.57 = bf16[5,1024,1,1,256]{1,4,0,3,2:T(8,128)(2,1)} copy(bf16[5,1024,1,1,256]{4,3,1,0,2:T(2,128)(2,1)} %constant_dynamic-slice_fusion.3) | data formatting | bytes 5242880 | tf_op jit(solution)/shard_map/jit(dynamic_index_in_dim)/dynamic_slice | solution.py:60
  763.0 11.7 %fusion.4 = f32[5,1,1,256,1024]{4,3,2,1,0:T(8,128)} fusion(f32[5,1,1,256,1024]{4,3,2,1,0:T(8,128)} %param.9, bf16[5,1024,1024]{1,2,0:T(8,128)(2,1)} %reshape.158, bf16[5,1024,1,1,256]{1,4,0,3,2:T(8,128)(2,1)} %copy.57), kind=kOutput, calls=%fused_computation.12 | convolution fusion | flops 2686976000 | bytes 23592960 | tf_op jit(solution)/shard_map/mnr,mnc->mrc/dot_general | solution.py:67
  774.6 9.6 fusion.5
  784.2 160.0 %all-to-all-done = bf16[8,5,256,1024]{3,2,1,0:T(8,128)(2,1)} async-done(((bf16[8,5,256,1024]{3,2,1,0:T(8,128)(2,1)}), bf16[8,5,256,1024]{3,2,1,0:T(8,128)(2,1)}, u32[]{:S(2)}, u32[]{:S(2)}) %all-to-all-start) | async-done | bytes 20971552 | tf_op jit(solution)/shard_map/all_to_all | solution.py:89
  944.2 21.6 %convert_bitcast_fusion = bf16[256,4,1024]{2,1,0:T(4,128)(2,1)} fusion(bf16[40,256,1024]{2,1,0:T(8,128)(2,1)} %bitcast.14, s32[4]{0:T(128)S(1)} %dynamic_slice.7), kind=kOutput, calls=%fused_computation.24 | convolution fusion | flops 84934816 | bytes 23068688 | tf_op jit(solution)/shard_map/cn,ntb->tcb/dot_general | solution.py:90
  965.8 4.5 reshape.164
  (45 shorter events, 4.6 us)
Async XLA Ops:
  7.2 484.7 %copy-start = (bf16[5,1,1,256,1024]{4,3,2,1,0:T(8,128)(2,1)S(1)}, bf16[5,1,1,256,1024]{4,3,2,1,0:T(8,128)(2,1)}, u32[]{:S(2)}) copy-start(bf16[5,1,1,256,1024]{4,3,2,1,0:T(8,128)(2,1)} %param.10) | copy-start | bytes 7864324
  7.2 150.5 %reduce-scatter.2.cloned.1.call-start = ((), (), s32[]{:S(2)}) async-start(), calls=%async_computation.2 | async-start | bytes 10485760 | tf_op jit(solution)/shard_map/reduce_scatter | solution.py:29
  7.2 150.6 %copy-start.5 = (s32[32]{0:T(128)S(1)}, s32[32]{0:T(128)}, u32[]{:S(2)}) copy-start(s32[32]{0:T(128)} %param.7) | copy-start | bytes 388
  7.2 151.0 %copy-start.4 = (s32[3]{0:T(128)S(1)}, s32[3]{0:T(128)}, u32[]{:S(2)}) copy-start(s32[3]{0:T(128)} %constant.68.clone.1) | copy-start | bytes 40
  7.9 242.1 %all-gather.9.cloned.1.call-start = ((), (), s32[]{:S(2)}) async-start(), calls=%async_computation.5 | async-start | bytes 18874368 | tf_op jit(solution)/shard_map/all_gather | solution.py:46
  157.7 299.2 %all-gather.5.cloned.1.call-start = ((), (), s32[]{:S(2)}) async-start(), calls=%async_computation.3 | async-start | bytes 13107200 | tf_op jit(solution)/shard_map/all_gather | solution.py:54
  272.9 367.6 %all-gather.7.cloned.1.call-start = ((), (), s32[]{:S(2)}) async-start(), calls=%async_computation.4 | async-start | bytes 13107200 | tf_op jit(solution)/shard_map/all_gather | solution.py:79
  649.8 7.4 copy-start.3
  709.2 235.0 %all-to-all-start = ((bf16[8,5,256,1024]{3,2,1,0:T(8,128)(2,1)}), bf16[8,5,256,1024]{3,2,1,0:T(8,128)(2,1)}, u32[]{:S(2)}, u32[]{:S(2)}) async-start(bf16[8,5,256,1024]{3,2,1,0:T(8,128)(2,1)} %bitcast.125), calls=%async_computation.1 | async-start | bytes 41943040 | tf_op jit(solution)/shard_map/all_to_all | solution.py:89
  763.0 11.7 %copy-start.2 = (bf16[5,1,256,1024]{3,2,1,0:T(8,128)(2,1)S(1)}, bf16[5,1,256,1024]{3,2,1,0:T(8,128)(2,1)}, u32[]{:S(2)}) copy-start(bf16[5,1,256,1024]{3,2,1,0:T(8,128)(2,1)} %get-tuple-element.10) | copy-start | bytes 7864324
  944.2 26.0 %copy-start.1 = (bf16[5,1,1,256,1024]{4,3,2,1,0:T(8,128)(2,1)S(1)}, bf16[5,1,1,256,1024]{4,3,2,1,0:T(8,128)(2,1)}, u32[]{:S(2)}) copy-start(bf16[5,1,1,256,1024]{4,3,2,1,0:T(8,128)(2,1)} %param.10) | copy-start | bytes 7864324
Sparse Core Ops, SparseCore 0:
  10.3 147.3 reduce-scatter.1
  159.6 90.3 all-gather.8
  273.1 183.8 all-gather.4
  458.4 182.0 all-gather.6
where the time goes:
time: 980 us; the launch traced here: 977 us
  waiting for transfers between devices  726 us (74%)
  local copies, waits for them, and re-layouts  129 us (13%)
  matrix products  60.5 us (6%)
  other arithmetic  40.4 us (4%)
  between operations  13.9 us (1%)
    all_gather x1, waiting for transfers between devices, on_device(): lax.all_gather(owned_rows, 'dp', axis=2, tiled=True)  183 us
    all_to_all x1, waiting for transfers between devices, on_device(): lax.all_to_all(homeward, 'fsdp', split_axis=0, concat_axis=0, tiled=True)  160 us
    reduce_scatter x1, waiting for transfers between devices, on_device(): lax.psum_scatter(replica_grads[0].astype(jnp.float32).astype(jnp.bfloat16...  150 us
    all_gather x1, waiting for transfers between devices, on_device(): lax.all_gather(right_inverse_root, 'dp', axis=2, tiled=True)  140 us
    all_gather x1, waiting for transfers between devices, on_device(): all_bands = lax.all_gather(summed[None], 'fsdp', axis=0, tiled=True)  91.7 us
    scatter x10, other arithmetic  36.5 us
    all_gather x2, local copies, waits for them, and re-layouts, on_device(): lax.all_gather(owned_rows, 'dp', axis=2, tiled=True)  27 us
    dot_general x1, matrix products, on_device(): jnp.einsum('cn,ntb->tcb', chooser, returned.reshape(total_slots, strip_ro...  21.6 us
  transfers between devices with their start and end apart: 5, of which 5 were waited for; matrix products, arithmetic and copies ran while one was open for 12% of the time, Pallas kernels for 0%

commit v1 on v0

--- a/solution.py
+++ b/solution.py
@@ -2,6 +2,19 @@
 import jax.numpy as jnp
 from jax import lax
 from jax.sharding import PartitionSpec as P
+from jax.lax import axis_index, axis_size, ppermute
+
+
+def form_levels_all(q_in, message):
+    arr_out, raw_out = (axis_size("dp"), axis_index("dp"))
+    copies = list(map(lambda no: (no, (no - 1) % arr_out), range(arr_out)))
+    lower = q_in.shape[2]
+    arr_now = q_in
+    z2 = message(arr_now, raw_out * lower)
+    for dd in range(1, arr_out):
+        arr_now = ppermute(arr_now, "dp", perm=copies)
+        z2 = z2 + message(arr_now, (raw_out + dd) % arr_out * lower)
+    return z2
 
 
 def on_device(
@@ -73,11 +86,14 @@
     mixed_split = mixed_rows.reshape(
         slots_here, sub_blocks * strip_rows, sub_blocks, groups, strip_rows
     )
-    result = jnp.einsum(
-        "mrqjt,mqjtc->mrc",
-        mixed_split,
-        lax.all_gather(right_inverse_root, "dp", axis=2, tiled=True),
-        preferred_element_type=jnp.float32,
+    result = form_levels_all(
+        right_inverse_root,
+        lambda shard, offset_2: jnp.einsum(
+            "mrqjt,mqjtc->mrc",
+            lax.dynamic_slice_in_dim(mixed_split, offset_2, shard.shape[2], axis=3),
+            shard,
+            preferred_element_type=jnp.float32,
+        ),
     )
     outcome = result.astype(jnp.bfloat16).reshape(slots_here, sub_blocks, strip_rows, block_size)
     homeward = jax.vmap(

time: 980 us -> 950 us (0.969)
  waiting for transfers between devices: 726 us -> 694 us
    ppermute x0 -> x3, waiting for transfers between devices: none -> 290 us  [form_levels_all(): arr_now = ppermute(arr_now, 'dp', perm=copies)]
    all_gather x1, waiting for transfers between devices: 183 us -> 1.52 us  [on_device(): lax.all_gather(owned_rows, 'dp', axis=2, tiled=True)]
    all_gather x1 -> x0, waiting for transfers between devices: 140 us -> none  [on_device(): lax.all_gather(right_inverse_root, 'dp', axis=2, tiled=True)]
  transfers between devices with their start and end apart: 5 -> 7, of which waited for: 5 -> 7; matrix products, arithmetic and copies ran while one was open for 12% -> 12% of each run, Pallas kernels for 0% -> 0%
where the time goes in v1:
time: 950 us; the launch traced here: 947 us
  waiting for transfers between devices  694 us (73%)
  local copies, waits for them, and re-layouts  131 us (14%)
  matrix products  58.9 us (6%)
  other arithmetic  39.8 us (4%)
  between operations  13.9 us (1%)
  starting transfers between devices  9.77 us (1%)
    ppermute x3, waiting for transfers between devices, form_levels_all(): arr_now = ppermute(arr_now, 'dp', perm=copies)  290 us
    all_to_all x1, waiting for transfers between devices, on_device(): lax.all_to_all(homeward, 'fsdp', split_axis=0, concat_axis=0, tiled=True)  160 us
    reduce_scatter x1, waiting for transfers between devices, on_device(): lax.psum_scatter(replica_grads[0].astype(jnp.float32).astype(jnp.bfloat16...  150 us
    all_gather x1, waiting for transfers between devices, on_device(): all_bands = lax.all_gather(summed[None], 'fsdp', axis=0, tiled=True)  91.7 us
    scatter x10, other arithmetic  35.9 us
    all_gather x2, local copies, waits for them, and re-layouts, on_device(): lax.all_gather(owned_rows, 'dp', axis=2, tiled=True)  26.6 us
    dot_general x1, matrix products, on_device(): jnp.einsum('cn,ntb->tcb', chooser, returned.reshape(total_slots, strip_ro...  21.6 us
    gather x15, local copies, waits for them, and re-layouts  20.3 us
  transfers between devices with their start and end apart: 7, of which 7 were waited for; matrix products, arithmetic and copies ran while one was open for 12% of the time, Pallas kernels for 0%

profile of v1, /device:TPU:0, one launch (start us, length us, event | category | flops | bytes accessed | tf_op | source)
XLA Modules:
  0.0 946.5 jit_solution(5097748173521850206)
XLA Ops:
  8.0 149.7 %reduce-scatter.2.cloned.1.call-done = bf16[256,4096]{1,0:T(8,128)(2,1)} async-done(((bf16[1024,4096]{1,0:T(8,128)(2,1)}), bf16[256,4096]{1,0:T(8,128)(2,1)}) %reduce-scatter.2.cloned.1.call-update) | async-done | bytes 2097168 | tf_op jit(solution)/shard_map/reduce_scatter | solution.py:42
  158.3 91.7 %all-gather.6.cloned.1.call-done = bf16[2048,4096]{1,0:T(8,128)(2,1)} async-done(((bf16[256,4096]{1,0:T(8,128)(2,1)}), bf16[2048,4096]{1,0:T(8,128)(2,1)}) %all-gather.6.cloned.1.call-update) | async-done | bytes 16777232 | tf_op jit(solution)/shard_map/all_gather | solution.py:59
  250.0 20.3 %while.2 = (s32[]{:T(128)}, bf16[8,256,4096]{2,1,0:T(8,128)(2,1)}, s32[5,3]{0,1:T(4,128)S(1)}, bf16[5,1,256,1024]{3,2,1,0:T(8,128)(2,1)}, s32[]{:T(128)}) while((s32[]{:T(128)}, bf16[8,256,4096]{2,1,0:T(8,128)(2,1)}, s32[5,3]{0,1:T(4,128)S(1)}, bf16[5,1,256,1024]{3,2,1,0:T(8,128)(2,1)}, s32[]{:T(128)}) %tuple.61), condition=%wide.while_cond, body=%wide.while_body.sunk | while | flops 2 | bytes 1049717 | solution.py:61
  250.6 3.4 bitcast_dynamic-update-slice_fusion.4
  254.7 3.4 bitcast_dynamic-update-slice_fusion.4
  258.8 3.4 bitcast_dynamic-update-slice_fusion.4
  262.8 3.4 bitcast_dynamic-update-slice_fusion.4
  266.9 3.4 bitcast_dynamic-update-slice_fusion.4
  270.3 3.5 bitcast_multiply_fusion.2
  273.8 3.4 collective-permute-start
  277.2 147.5 %collective-permute-done = bf16[5,1,1,256,1024]{4,3,0,2,1:T(8,128)(2,1)S(1)} collective-permute-done((bf16[5,1,1,256,1024]{4,3,0,2,1:T(8,128)(2,1)}, bf16[5,1,1,256,1024]{4,3,0,2,1:T(8,128)(2,1)S(1)}, u32[]{:S(2)}, u32[]{:S(2)}) %collective-permute-start) | collective-permute-done | bytes 2621472 | tf_op jit(solution)/shard_map/ppermute | solution.py:15
  424.7 1.5 copy-done.4
  426.2 131.7 %collective-permute-done.1 = bf16[5,1,1,256,1024]{4,3,0,2,1:T(8,128)(2,1)} collective-permute-done((bf16[5,1,1,256,1024]{4,3,0,2,1:T(8,128)(2,1)S(1)}, bf16[5,1,1,256,1024]{4,3,0,2,1:T(8,128)(2,1)}, u32[]{:S(2)}, u32[]{:S(2)}) %collective-permute-start.1) | collective-permute-done | bytes 2621472 | tf_op jit(solution)/shard_map/ppermute | solution.py:15
  557.9 1.5 all-gather.4.cloned.1.call-done
  559.4 17.0 %copy.57 = bf16[5,1,4,256,1024]{3,2,4,0,1:T(4,128)(2,1)} copy(bf16[5,1,4,256,1024]{4,3,1,0,2:T(8,128)(2,1)} %all-gather.4.cloned.1.call-done) | data formatting | bytes 20971520 | tf_op jit(solution)/shard_map/all_gather | solution.py:67
  576.4 17.5 %reshape.177 = bf16[5,1024,1024]{1,2,0:T(8,128)(2,1)} reshape(bf16[5,1,4,256,1024]{3,2,4,0,1:T(4,128)(2,1)} %copy.57) | data formatting | bytes 20971520 | tf_op jit(solution)/shard_map/reshape | solution.py:67
  593.9 7.0 fusion.22
  601.0 0.9 fusion.14
  601.9 2.8 fusion.10
  605.6 10.7 %collective-permute-done.2 = bf16[5,1,1,256,1024]{4,3,0,2,1:T(8,128)(2,1)} collective-permute-done((bf16[5,1,1,256,1024]{4,3,0,2,1:T(8,128)(2,1)}, bf16[5,1,1,256,1024]{4,3,0,2,1:T(8,128)(2,1)}, u32[]{:S(2)}, u32[]{:S(2)}) %collective-permute-start.2) | collective-permute-done | bytes 2621472 | tf_op jit(solution)/shard_map/ppermute | solution.py:15
  616.4 4.5 fusion.4
  620.9 7.4 broadcast_in_dim.18.clone
  628.2 50.8 %while.3 = (s32[]{:T(128)}, bf16[5,8,256,1024]{3,2,0,1:T(8,128)(2,1)}, s32[5,4]{0,1:T(4,128)S(1)}, bf16[5,1,256,1024]{3,2,1,0:T(8,128)(2,1)}, s32[]{:T(128)}, /*index=5*/s32[4]{0:T(128)S(1)}) while((s32[]{:T(128)}, bf16[5,8,256,1024]{3,2,0,1:T(8,128)(2,1)}, s32[5,4]{0,1:T(4,128)S(1)}, bf16[5,1,256,1024]{3,2,1,0:T(8,128)(2,1)}, s32[]{:T(128)}, ...), condition=%wide.while_cond.1, body=%wide.while_body.1.sunk | while | flops 262173 | bytes 2623166 | solution.py:100
  628.9 3.2 and_reduce_fusion.2
  632.1 2.3 constant_dynamic-slice_fusion.9
  634.4 4.0 bitcast_dynamic-update-slice_fusion.5
  639.1 3.2 and_reduce_fusion.2
  642.3 2.3 constant_dynamic-slice_fusion.9
  644.6 4.0 bitcast_dynamic-update-slice_fusion.5
  649.2 3.2 and_reduce_fusion.2
  652.4 2.3 constant_dynamic-slice_fusion.9
  654.7 4.0 bitcast_dynamic-update-slice_fusion.5
  659.4 3.2 and_reduce_fusion.2
  662.6 2.3 constant_dynamic-slice_fusion.9
  664.9 4.0 bitcast_dynamic-update-slice_fusion.5
  669.6 3.2 and_reduce_fusion.2
  672.8 2.3 constant_dynamic-slice_fusion.9
  675.1 4.0 bitcast_dynamic-update-slice_fusion.5
  679.0 6.3 all-to-all-start
  685.4 9.7 %copy.68 = bf16[5,1,4,256,1024]{4,3,2,0,1:T(8,128)(2,1)} copy(bf16[5,1,4,256,1024]{4,3,1,0,2:T(8,128)(2,1)} %all-gather.4.cloned.1.call-done) | data formatting | bytes 20971520 | tf_op jit(solution)/shard_map/all_gather | solution.py:67
  695.1 17.9 %reshape_reshape.4 = bf16[5,1024,1,4,256]{4,3,1,0,2:T(4,128)(2,1)} reshape(bf16[5,1,4,256,1024]{4,3,2,0,1:T(8,128)(2,1)} %copy.68) | data formatting | bytes 20971520 | tf_op jit(solution)/shard_map/reshape;reshape | solution.py:74
  712.9 8.7 constant_dynamic-slice_fusion.3
  721.6 11.1 %copy.69 = bf16[5,1024,1,1,256]{1,4,0,3,2:T(8,128)(2,1)} copy(bf16[5,1024,1,1,256]{4,3,1,0,2:T(2,128)(2,1)} %constant_dynamic-slice_fusion.3) | data formatting | bytes 5242880 | tf_op jit(solution)/shard_map/jit(dynamic_index_in_dim)/dynamic_slice | solution.py:73
  732.8 11.7 %fusion.2 = f32[5,1,1,256,1024]{4,3,2,1,0:T(8,128)} fusion(f32[5,1,1,256,1024]{4,3,2,1,0:T(8,128)} %param.9, bf16[5,1024,1024]{1,2,0:T(8,128)(2,1)} %reshape.177, bf16[5,1024,1,1,256]{1,4,0,3,2:T(8,128)(2,1)} %copy.69), kind=kOutput, calls=%fused_computation.10 | convolution fusion | flops 2686976000 | bytes 23592960 | tf_op jit(solution)/shard_map/mnr,mnc->mrc/dot_general | solution.py:80
  744.4 9.6 %fusion.3 = f32[5,1,1,256,1024]{4,3,2,1,0:T(8,128)} fusion(f32[5,1,1,256,1024]{4,3,2,1,0:T(8,128)} %param.8, bf16[5,1024,1024]{1,2,0:T(8,128)(2,1)} %reshape.177, bf16[5,1,256,1024]{3,2,1,0:T(8,128)(2,1)S(1)} %copy-done.2, bf16[5]{0:T(256)(128)(2,1)S(1)} %convert_element_type.26), kind=kOutput, calls=%fused_computation.12 | convolution fusion | flops 2688286720 | bytes 23592970 | tf_op jit(solution)/shard_map/mrc,mnc->mrn/dot_general | solution.py:71
  754.0 160.0 %all-to-all-done = bf16[8,5,256,1024]{3,2,1,0:T(8,128)(2,1)} async-done(((bf16[8,5,256,1024]{3,2,1,0:T(8,128)(2,1)}), bf16[8,5,256,1024]{3,2,1,0:T(8,128)(2,1)}, u32[]{:S(2)}, u32[]{:S(2)}) %all-to-all-start) | async-done | bytes 20971552 | tf_op jit(solution)/shard_map/all_to_all | solution.py:105
  914.0 21.6 %convert_bitcast_fusion = bf16[256,4,1024]{2,1,0:T(4,128)(2,1)} fusion(bf16[40,256,1024]{2,1,0:T(8,128)(2,1)} %bitcast.20, s32[4]{0:T(128)S(1)} %dynamic_slice.23), kind=kOutput, calls=%fused_computation.30 | convolution fusion | flops 84934816 | bytes 23068688 | tf_op jit(solution)/shard_map/cn,ntb->tcb/dot_general | solution.py:106
  935.6 4.5 reshape.190
  (57 shorter events, 9.0 us)
Async XLA Ops:
  7.2 586.8 %copy-start = (bf16[5,1,1,256,1024]{4,3,2,1,0:T(8,128)(2,1)S(1)}, bf16[5,1,1,256,1024]{4,3,2,1,0:T(8,128)(2,1)}, u32[]{:S(2)}) copy-start(bf16[5,1,1,256,1024]{4,3,2,1,0:T(8,128)(2,1)} %param.10) | copy-start | bytes 7864324
  7.2 150.5 %reduce-scatter.2.cloned.1.call-start = ((), (), s32[]{:S(2)}) async-start(), calls=%async_computation.2 | async-start | bytes 10485760 | tf_op jit(solution)/shard_map/reduce_scatter | solution.py:42
  7.2 150.6 %copy-start.8 = (s32[32]{0:T(128)S(1)}, s32[32]{0:T(128)}, u32[]{:S(2)}) copy-start(s32[32]{0:T(128)} %param.7) | copy-start | bytes 388
  7.2 151.0 %copy-start.7 = (s32[3]{0:T(128)S(1)}, s32[3]{0:T(128)}, u32[]{:S(2)}) copy-start(s32[3]{0:T(128)} %constant.85.clone.1) | copy-start | bytes 40
  7.9 242.1 %all-gather.6.cloned.1.call-start = ((), (), s32[]{:S(2)}) async-start(), calls=%async_computation.4 | async-start | bytes 18874368 | tf_op jit(solution)/shard_map/all_gather | solution.py:59
  157.7 401.7 %all-gather.4.cloned.1.call-start = ((), (), s32[]{:S(2)}) async-start(), calls=%async_computation.3 | async-start | bytes 13107200 | tf_op jit(solution)/shard_map/all_gather | solution.py:67
  273.8 150.9 %collective-permute-start = (bf16[5,1,1,256,1024]{4,3,0,2,1:T(8,128)(2,1)}, bf16[5,1,1,256,1024]{4,3,0,2,1:T(8,128)(2,1)S(1)}, u32[]{:S(2)}, u32[]{:S(2)}) collective-permute-start(bf16[5,1,1,256,1024]{4,3,0,2,1:T(8,128)(2,1)} %bitcast.150), channel_id=1, source_target_pairs={{0,24},{8,0},{16,8},{24,16},{1,25},{9,1},{17,9},{25,17},{2,26},{10... | collective-permute-start | bytes 7864328 | tf_op jit(solution)/shard_map/ppermute | solution.py:15
  424.7 1.5 copy-start.4
  426.2 131.7 %collective-permute-start.1 = (bf16[5,1,1,256,1024]{4,3,0,2,1:T(8,128)(2,1)S(1)}, bf16[5,1,1,256,1024]{4,3,0,2,1:T(8,128)(2,1)}, u32[]{:S(2)}, u32[]{:S(2)}) collective-permute-start(bf16[5,1,1,256,1024]{4,3,0,2,1:T(8,128)(2,1)S(1)} %collective-permute-done), channel_id=1, source_target_pairs={{0,24},{8,0},{16,8},{24,16},{1,25},{9,1},{17,9},{25,17},{2,26},{10... | collective-permute-start | bytes 7864328 | tf_op jit(solution)/shard_map/ppermute | solution.py:15
  557.9 58.5 %collective-permute-start.2 = (bf16[5,1,1,256,1024]{4,3,0,2,1:T(8,128)(2,1)}, bf16[5,1,1,256,1024]{4,3,0,2,1:T(8,128)(2,1)}, u32[]{:S(2)}, u32[]{:S(2)}) collective-permute-start(bf16[5,1,1,256,1024]{4,3,0,2,1:T(8,128)(2,1)} %collective-permute-done.1), channel_id=1, source_target_pairs={{0,24},{8,0},{16,8},{24,16},{1,25},{9,1},{17,9},{25,17},{2,26},{10... | collective-permute-start | bytes 7864328 | tf_op jit(solution)/shard_map/ppermute | solution.py:15
  593.9 7.0 copy-start.3
  601.9 2.8 copy-start.5
  620.9 7.4 copy-start.6
  679.0 235.0 %all-to-all-start = ((bf16[8,5,256,1024]{3,2,1,0:T(8,128)(2,1)}), bf16[8,5,256,1024]{3,2,1,0:T(8,128)(2,1)}, u32[]{:S(2)}, u32[]{:S(2)}) async-start(bf16[8,5,256,1024]{3,2,1,0:T(8,128)(2,1)} %bitcast.144), calls=%async_computation.1 | async-start | bytes 41943040 | tf_op jit(solution)/shard_map/all_to_all | solution.py:105
  732.7 11.7 %copy-start.2 = (bf16[5,1,256,1024]{3,2,1,0:T(8,128)(2,1)S(1)}, bf16[5,1,256,1024]{3,2,1,0:T(8,128)(2,1)}, u32[]{:S(2)}) copy-start(bf16[5,1,256,1024]{3,2,1,0:T(8,128)(2,1)} %get-tuple-element.10) | copy-start | bytes 7864324
  914.0 26.0 %copy-start.1 = (bf16[5,1,1,256,1024]{4,3,2,1,0:T(8,128)(2,1)S(1)}, bf16[5,1,1,256,1024]{4,3,2,1,0:T(8,128)(2,1)}, u32[]{:S(2)}) copy-start(bf16[5,1,1,256,1024]{4,3,2,1,0:T(8,128)(2,1)} %param.10) | copy-start | bytes 7864324
Sparse Core Ops, SparseCore 0:
  10.3 147.3 reduce-scatter.1
  159.6 90.3 all-gather.5
  273.9 285.4 all-gather.3
